TPU v7x, 128 devices: a whole 4x4x4 slice. The times are simulated.
128 devices in a mesh: row: 8 (over x, y_lo), col: 16 (over y_hi, z, core).
Axes of the slice: x: 4, y: 4 (y_hi: 2, y_lo: 2; y = y_hi * 2 + y_lo), z: 4, core: 2. Of those that a mesh axis runs over, the one named last changes fastest.
Arguments:
- train_table: bfloat16 [8, 256, 262144], P('row', 'col'), may hold values from -6 to 6
- token_ids: int32 [512], replicated, may hold values from 0 to 262143
- hidden: bfloat16 [8, 512, 2560], P('row', 'col'), may hold values from -6 to 6
- w_gate: bfloat16 [8, 2560, 256], P('row'), may hold values from -0.125 to 0.125
- w_proj: bfloat16 [8, 256, 2560], P('row'), may hold values from -0.375 to 0.375
- gain: bfloat16 [8, 2560], P('row'), may hold values from 0.5 to 1.5
Outputs:
- serve_table: bfloat16 [8, 256, 262144], P(None, None, ('row', 'col'))
- update: bfloat16 [8, 512, 2560], P('row', 'col')
All inputs are finite; a program needn't handle non-finite values.
Results may differ from a plain program's by a relative error of at most 0.0048.
Values may be sent and summed in bfloat16 or wider, within the bound.
No kernel may reach another device: no remote copies, remote signals or barrier semaphores. Data moves between devices by JAX's collectives and lax.ppermute only.
A program may use at most 256 MiB of HBM per device.

v0:
```python
import jax
import jax.numpy as jnp
from jax import lax
from jax.sharding import PartitionSpec as P


def shards(train_table, token_ids, hidden, w_gate, w_proj, gain):
    row_count = lax.axis_size("row")
    col_count = lax.axis_size("col")
    devices_all = row_count * col_count
    columns = train_table.shape[1]
    local_vocab = train_table.shape[2] // devices_all
    shaped = train_table.reshape(columns, devices_all, local_vocab)
    arrived = lax.all_to_all(shaped, ("row", "col"), split_axis=1, concat_axis=0, tiled=True)
    served = arrived.reshape(row_count, col_count * columns, local_vocab)
    picked = jnp.take(train_table[0], token_ids, axis=1)
    picked = picked.reshape(columns, col_count, picked.shape[1] // col_count)
    owned = lax.all_to_all(picked, "col", split_axis=1, concat_axis=0, tiled=True)
    owned = owned.reshape(owned.shape[0], owned.shape[2])
    emb = jnp.transpose(owned).astype(jnp.float32)
    current = hidden[0]
    gate_pre = jnp.dot(current, w_gate[0], preferred_element_type=jnp.float32)
    gated = jax.nn.gelu(gate_pre, approximate=True)
    mixed = (gated * emb).astype(jnp.bfloat16)
    projected = jnp.dot(mixed, w_proj[0], preferred_element_type=jnp.float32)
    inverse_rms = lax.rsqrt(jnp.mean(projected * projected, axis=-1, keepdims=True) + 1e-06)
    update = (projected * inverse_rms * gain[0].astype(jnp.float32)[None, :]).astype(jnp.bfloat16)
    return (served, update[None])


def solution(mesh):
    in_specs = (
        P("row", "col", None),
        P(),
        P("row", "col", None),
        P("row", None, None),
        P("row", None, None),
        P("row", None),
    )
    out_specs = (P(None, None, ("row", "col")), P("row", "col", None))
    return jax.shard_map(shards, mesh=mesh, in_specs=in_specs, out_specs=out_specs, check_vma=False)
```

profile of v0, /device:TPU:6, one launch (start us, length us, event | category | flops | bytes accessed | tf_op | source)
XLA Modules:
  0.0 206.7 jit_solution(7989710100247783820)
XLA Ops:
  0.6 0.0 copy-start
  0.6 0.8 compare_select_fusion
  1.4 0.7 compare_and_fusion
  2.1 44.6 %copy.12 = bf16[1,16,262144]{1,2,0:T(8,128)(2,1)} copy(bf16[1,16,262144]{2,1,0:T(8,128)(2,1)} %param.6) | data formatting | bytes 16777216 | tf_op args[0]
  46.7 3.6 %gather_fusion = bf16[512,16]{1,0:T(8,128)(2,1)S(1)} fusion(bf16[16,262144]{0,1:T(8,128)(2,1)} %bitcast.5, s32[1024]{0:T(1024)S(1)} %pad_clamp_fusion), kind=kCustom, calls=%fused_computation | custom fusion | bytes 34816 | tf_op jit(solution)/shard_map/jit(_take)/gather | solution.py:16
  50.3 0.1 copy.13
  50.4 0.1 broadcast_in_dim.19
  50.5 0.7 reshape.52
  51.2 8.0 %all-to-all-start.1 = ((bf16[16,2,256]{2,1,0:T(2,128)(2,1)}), bf16[16,2,256]{2,1,0:T(2,128)(2,1)S(1)}, u32[]{:S(2)}, u32[]{:S(2)}) async-start(bf16[16,2,256]{2,1,0:T(2,128)(2,1)} %reshape.52), calls=%async_computation.1 | async-start | bytes 32768 | tf_op jit(solution)/shard_map/all_to_all | solution.py:18
  59.3 11.4 %copy.15 = bf16[2,8,128,2048]{3,2,1,0:T(8,128)(2,1)} copy(bf16[2,8,128,2048]{3,1,2,0:T(8,128)(2,1)} %bitcast.62) | data formatting | bytes 16777216
  70.7 11.2 %copy.11 = bf16[16,128,2048]{2,0,1:T(8,128)(2,1)} copy(bf16[16,128,2048]{2,1,0:T(8,128)(2,1)} %bitcast.63) | data formatting | bytes 16777216 | tf_op jit(solution)/shard_map/reshape | solution.py:13
  82.0 0.0 copy-start.3
  82.0 0.0 copy-start.1
  82.0 0.0 copy-start.2
  82.0 0.0 all-to-all-done.1
  82.0 10.1 %all-to-all-start = ((bf16[16,128,2048]{2,0,1:T(8,128)(2,1)}), bf16[16,128,2048]{2,0,1:T(8,128)(2,1)}, u32[]{:S(2)}, u32[]{:S(2)}) async-start(bf16[16,128,2048]{2,0,1:T(8,128)(2,1)} %copy.11), calls=%async_computation | async-start | bytes 16777216 | tf_op jit(solution)/shard_map/all_to_all | solution.py:14
  92.1 0.0 copy-done.3
  92.1 0.1 reshape.53
  92.3 0.1 copy.14
  92.3 0.0 copy-done
  92.3 0.0 copy-done.1
  92.3 0.0 copy-done.2
  92.3 1.0 multiply_reduce_fusion
  93.4 0.8 fusion.4
  94.1 104.1 %all-to-all-done = bf16[16,128,2048]{2,0,1:T(8,128)(2,1)} async-done(((bf16[16,128,2048]{2,0,1:T(8,128)(2,1)}), bf16[16,128,2048]{2,0,1:T(8,128)(2,1)}, u32[]{:S(2)}, u32[]{:S(2)}) %all-to-all-start) | async-done | bytes 8388640 | tf_op jit(solution)/shard_map/all_to_all | solution.py:14
  198.2 8.4 %copy.17 = bf16[8,256,2048]{2,1,0:T(8,128)(2,1)} copy(bf16[8,256,2048]{2,1,0:T(8,128)(2,1)} %bitcast.2) | data formatting | bytes 16777216
  (5 shorter events, 0.1 us)
Async XLA Ops:
  0.6 91.7 %copy-start = (bf16[1,256,2560]{2,1,0:T(8,128)(2,1)S(1)}, bf16[1,256,2560]{2,1,0:T(8,128)(2,1)}, u32[]{:S(2)}) copy-start(bf16[1,256,2560]{2,1,0:T(8,128)(2,1)} %param.10) | copy-start | bytes 3932164
  51.2 30.7 %all-to-all-start.1 = ((bf16[16,2,256]{2,1,0:T(2,128)(2,1)}), bf16[16,2,256]{2,1,0:T(2,128)(2,1)S(1)}, u32[]{:S(2)}, u32[]{:S(2)}) async-start(bf16[16,2,256]{2,1,0:T(2,128)(2,1)} %reshape.52), calls=%async_computation.1 | async-start | bytes 32768 | tf_op jit(solution)/shard_map/all_to_all | solution.py:18
  82.0 10.1 %copy-start.3 = (bf16[1,2560]{1,0:T(2,128)(2,1)S(1)}, bf16[1,2560]{1,0:T(2,128)(2,1)}, u32[]{:S(2)}) copy-start(bf16[1,2560]{1,0:T(2,128)(2,1)} %param.11) | copy-start | bytes 15364
  82.0 10.4 %copy-start.1 = (bf16[1,2560,256]{2,1,0:T(8,128)(2,1)S(1)}, bf16[1,2560,256]{2,1,0:T(8,128)(2,1)}, u32[]{:S(2)}) copy-start(bf16[1,2560,256]{2,1,0:T(8,128)(2,1)} %param.9) | copy-start | bytes 3932164
  82.0 10.4 %copy-start.2 = (bf16[1,32,2560]{2,1,0:T(8,128)(2,1)S(1)}, bf16[1,32,2560]{2,1,0:T(8,128)(2,1)}, u32[]{:S(2)}) copy-start(bf16[1,32,2560]{2,1,0:T(8,128)(2,1)} %param.8) | copy-start | bytes 491524
  82.0 116.2 %all-to-all-start = ((bf16[16,128,2048]{2,0,1:T(8,128)(2,1)}), bf16[16,128,2048]{2,0,1:T(8,128)(2,1)}, u32[]{:S(2)}, u32[]{:S(2)}) async-start(bf16[16,128,2048]{2,0,1:T(8,128)(2,1)} %copy.11), calls=%async_computation | async-start | bytes 16777216 | tf_op jit(solution)/shard_map/all_to_all | solution.py:14
where the time goes:
time: 208 us; the launch traced here: 207 us
  waiting for transfers between devices  104 us (50%)
  local copies, waits for them, and re-layouts  80.4 us (39%)
  starting transfers between devices  18.2 us (9%)
  other arithmetic  2.33 us (1%)
    all_to_all x1, waiting for transfers between devices, shards(): lax.all_to_all(shaped, ('row', 'col'), split_axis=1, concat_axis=0, tiled...  104 us
    unnamed x13, local copies, waits for them, and re-layouts  65.3 us
    reshape x1, local copies, waits for them, and re-layouts, shards(): shaped = train_table.reshape(columns, devices_all, local_vocab)  11.2 us
    all_to_all x1, starting transfers between devices, shards(): lax.all_to_all(shaped, ('row', 'col'), split_axis=1, concat_axis=0, tiled...  10.1 us
    all_to_all x1, starting transfers between devices, shards(): lax.all_to_all(picked, 'col', split_axis=1, concat_axis=0, tiled=True)  8.05 us
  transfers between devices with their start and end apart: 2, of which 1 were waited for; matrix products, arithmetic and copies ran while one was open for 12% of the time, Pallas kernels for 0%

commit v1 on v0

--- a/solution.py
+++ b/solution.py
@@ -1,7 +1,47 @@
 import jax
 import jax.numpy as jnp
 from jax import lax
+from jax.experimental import pallas as pl
+from jax.experimental.pallas import tpu as pltpu
 from jax.sharding import PartitionSpec as P
+
+LANES = 128
+
+
+def pick_kernel(ids_ref, table_ref, out_ref, tiles, sem):
+    tokens = ids_ref.shape[0]
+    columns = table_ref.shape[1]
+
+    @pl.loop(0, tokens, unroll=8)
+    def _(t):
+        start = pl.multiple_of((ids_ref[t] // LANES) * LANES, LANES)
+        pltpu.make_async_copy(table_ref.at[0, :, pl.ds(start, LANES)], tiles.at[t], sem).start()
+
+    pltpu.make_async_copy(tiles, tiles, sem).wait()
+    lane = lax.broadcasted_iota(jnp.int32, (columns, LANES), 1)
+    for block in range(tokens // LANES):
+
+        def step(i, acc):
+            t = block * LANES + i
+            at = ids_ref[t] % LANES
+            turned = pltpu.roll(tiles[t].astype(jnp.float32), (i - at + LANES) % LANES, 1)
+            return jnp.where(lane == i, turned, acc)
+
+        acc = lax.fori_loop(0, LANES, step, jnp.zeros((columns, LANES), jnp.float32), unroll=8)
+        out_ref[:, block * LANES:(block + 1) * LANES] = acc.astype(jnp.bfloat16)
+
+
+def pick_columns(token_ids, train_table):
+    tokens = token_ids.shape[0]
+    columns = train_table.shape[1]
+    return pl.pallas_call(
+        pick_kernel,
+        out_shape=jax.ShapeDtypeStruct((columns, tokens), jnp.bfloat16),
+        in_specs=[pl.BlockSpec(memory_space=pltpu.SMEM), pl.BlockSpec(memory_space=pl.ANY)],
+        out_specs=pl.BlockSpec(memory_space=pltpu.VMEM),
+        scratch_shapes=[pltpu.VMEM((tokens, columns, LANES), jnp.bfloat16), pltpu.SemaphoreType.DMA],
+        cost_estimate=pl.CostEstimate(flops=20_000_000, bytes_accessed=2 << 20, transcendentals=0),
+    )(token_ids, train_table)
 
 
 def shards(train_table, token_ids, hidden, w_gate, w_proj, gain):
@@ -10,10 +50,11 @@
     devices_all = row_count * col_count
     columns = train_table.shape[1]
     local_vocab = train_table.shape[2] // devices_all
-    shaped = train_table.reshape(columns, devices_all, local_vocab)
-    arrived = lax.all_to_all(shaped, ("row", "col"), split_axis=1, concat_axis=0, tiled=True)
+    shaped = train_table.reshape(columns // 8, 8, devices_all, local_vocab)
+    shaped = jnp.transpose(shaped, (2, 0, 1, 3))
+    arrived = lax.all_to_all(shaped, ("row", "col"), split_axis=0, concat_axis=0, tiled=True)
     served = arrived.reshape(row_count, col_count * columns, local_vocab)
-    picked = jnp.take(train_table[0], token_ids, axis=1)
+    picked = pick_columns(token_ids, train_table)
     picked = picked.reshape(columns, col_count, picked.shape[1] // col_count)
     owned = lax.all_to_all(picked, "col", split_axis=1, concat_axis=0, tiled=True)
     owned = owned.reshape(owned.shape[0], owned.shape[2])

time: 208 us -> 157 us (0.75)
  local copies, waits for them, and re-layouts: 80.4 us -> 18.6 us
  Pallas kernels: 0 us -> 13.2 us
    unnamed x13 -> x11, local copies, waits for them, and re-layouts: 65.3 us -> 9.28 us
    pallas_call x0 -> x1, Pallas kernels: none -> 13.2 us  [pick_columns(): pl.pallas_call(pick_kernel, out_shape=jax.ShapeDtypeStruct((columns, toke...]
    gather x2 -> x0, local copies, waits for them, and re-layouts: 3.7 us -> none  [shards(): picked = jnp.take(train_table[0], token_ids, axis=1)]
    reshape x1 -> x3, local copies, waits for them, and re-layouts: 11.2 us -> 9.29 us  [the longest x1 8.44 us: shards(): shaped = train_table.reshape(columns // 8, 8, devices_all, local_vocab)]
  transfers between devices with their start and end apart: 2 -> 2, of which waited for: 1 -> 1; matrix products, arithmetic and copies ran while one was open for 12% -> 7% of each run, Pallas kernels for 0% -> 0%
where the time goes in v1:
time: 157 us
  waiting for transfers between devices  104 us (66%)
  local copies, waits for them, and re-layouts  18.6 us (12%)
  starting transfers between devices  18.2 us (12%)
  Pallas kernels  13.2 us (8%)
    all_to_all x1, waiting for transfers between devices, shards(): lax.all_to_all(shaped, ('row', 'col'), split_axis=0, concat_axis=0, tiled...  104 us
    pallas_call x1, Pallas kernels, pick_columns(): pl.pallas_call(pick_kernel, out_shape=jax.ShapeDtypeStruct((columns, toke...  13.2 us
    all_to_all x1, starting transfers between devices, shards(): lax.all_to_all(shaped, ('row', 'col'), split_axis=0, concat_axis=0, tiled...  10.1 us
    unnamed x11, local copies, waits for them, and re-layouts  9.28 us
    reshape x1, local copies, waits for them, and re-layouts, shards(): shaped = train_table.reshape(columns // 8, 8, devices_all, local_vocab)  8.44 us
    all_to_all x1, starting transfers between devices, shards(): lax.all_to_all(picked, 'col', split_axis=1, concat_axis=0, tiled=True)  8.05 us
  transfers between devices with their start and end apart: 2, of which 1 were waited for; matrix products, arithmetic and copies ran while one was open for 7% of the time, Pallas kernels for 0%

profile of v1, /device:TPU:6, one launch (start us, length us, event | category | flops | bytes accessed | tf_op | source)
XLA Modules:
  0.0 156.7 jit_solution(17931846725548664412)
XLA Ops:
  0.6 0.0 copy-start
  0.6 13.2 %shard_map.77 = bf16[16,512]{1,0:T(8,128)(2,1)} custom-call(s32[512]{0:T(512)} %ids_ref.1, bf16[1,16,262144]{2,1,0:T(8,128)(2,1)} %table_ref.1), custom_call_target="tpu_custom_call" | custom-call | flops 20000000 | bytes 2097152 | tf_op jit(solution)/shard_map/pallas_call | solution.py:37
  13.9 0.8 reshape.29
  14.8 0.7 reshape.34
  15.5 8.0 %all-to-all-start.1 = ((bf16[16,2,256]{2,1,0:T(2,128)(2,1)}), bf16[16,2,256]{2,1,0:T(2,128)(2,1)S(1)}, u32[]{:S(2)}, u32[]{:S(2)}) async-start(bf16[16,2,256]{2,1,0:T(2,128)(2,1)} %reshape.34), calls=%async_computation.1 | async-start | bytes 32768 | tf_op jit(solution)/shard_map/all_to_all | solution.py:59
  23.5 8.4 %copy.15 = bf16[2,8,128,2048]{3,1,0,2:T(8,128)(2,1)} copy(bf16[2,8,128,2048]{3,1,2,0:T(8,128)(2,1)} %bitcast.56) | data formatting | bytes 16777216 | tf_op jit(solution)/shard_map/reshape | solution.py:53
  32.0 0.0 all-to-all-done.1
  32.0 0.0 copy-start.3
  32.0 0.0 copy-start.1
  32.0 0.0 copy-start.2
  32.0 10.1 %all-to-all-start = ((bf16[128,2,8,2048]{3,2,1,0:T(8,128)(2,1)}), bf16[128,2,8,2048]{3,2,1,0:T(8,128)(2,1)}, u32[]{:S(2)}, u32[]{:S(2)}) async-start(bf16[128,2,8,2048]{3,2,1,0:T(8,128)(2,1)} %bitcast.57), calls=%async_computation | async-start | bytes 16777216 | tf_op jit(solution)/shard_map/all_to_all | solution.py:55
  42.1 0.0 copy-done.3
  42.1 0.1 reshape.35
  42.3 0.1 copy.12
  42.3 0.0 copy-done
  42.3 0.0 copy-done.1
  42.4 0.0 copy-done.2
  42.4 1.0 multiply_reduce_fusion
  43.4 0.8 fusion.4
  44.2 104.1 %all-to-all-done = bf16[128,2,8,2048]{3,2,1,0:T(8,128)(2,1)} async-done(((bf16[128,2,8,2048]{3,2,1,0:T(8,128)(2,1)}), bf16[128,2,8,2048]{3,2,1,0:T(8,128)(2,1)}, u32[]{:S(2)}, u32[]{:S(2)}) %all-to-all-start) | async-done | bytes 8388640 | tf_op jit(solution)/shard_map/all_to_all | solution.py:55
  148.2 8.4 %copy.18 = bf16[8,256,2048]{2,1,0:T(8,128)(2,1)} copy(bf16[8,256,2048]{2,1,0:T(8,128)(2,1)} %bitcast.2) | data formatting | bytes 16777216
  (4 shorter events, 0.1 us)
Async XLA Ops:
  0.6 41.7 %copy-start = (bf16[1,256,2560]{2,1,0:T(8,128)(2,1)S(1)}, bf16[1,256,2560]{2,1,0:T(8,128)(2,1)}, u32[]{:S(2)}) copy-start(bf16[1,256,2560]{2,1,0:T(8,128)(2,1)} %param.10) | copy-start | bytes 3932164
  15.5 16.5 %all-to-all-start.1 = ((bf16[16,2,256]{2,1,0:T(2,128)(2,1)}), bf16[16,2,256]{2,1,0:T(2,128)(2,1)S(1)}, u32[]{:S(2)}, u32[]{:S(2)}) async-start(bf16[16,2,256]{2,1,0:T(2,128)(2,1)} %reshape.34), calls=%async_computation.1 | async-start | bytes 32768 | tf_op jit(solution)/shard_map/all_to_all | solution.py:59
  32.0 10.1 %copy-start.3 = (bf16[1,2560]{1,0:T(2,128)(2,1)S(1)}, bf16[1,2560]{1,0:T(2,128)(2,1)}, u32[]{:S(2)}) copy-start(bf16[1,2560]{1,0:T(2,128)(2,1)} %param.11) | copy-start | bytes 15364
  32.0 10.4 %copy-start.1 = (bf16[1,2560,256]{2,1,0:T(8,128)(2,1)S(1)}, bf16[1,2560,256]{2,1,0:T(8,128)(2,1)}, u32[]{:S(2)}) copy-start(bf16[1,2560,256]{2,1,0:T(8,128)(2,1)} %param.9) | copy-start | bytes 3932164
  32.0 10.4 %copy-start.2 = (bf16[1,32,2560]{2,1,0:T(8,128)(2,1)S(1)}, bf16[1,32,2560]{2,1,0:T(8,128)(2,1)}, u32[]{:S(2)}) copy-start(bf16[1,32,2560]{2,1,0:T(8,128)(2,1)} %param.8) | copy-start | bytes 491524
  32.0 116.2 %all-to-all-start = ((bf16[128,2,8,2048]{3,2,1,0:T(8,128)(2,1)}), bf16[128,2,8,2048]{3,2,1,0:T(8,128)(2,1)}, u32[]{:S(2)}, u32[]{:S(2)}) async-start(bf16[128,2,8,2048]{3,2,1,0:T(8,128)(2,1)} %bitcast.57), calls=%async_computation | async-start | bytes 16777216 | tf_op jit(solution)/shard_map/all_to_all | solution.py:55

commit v2 on v0

v2 whole, which is shorter than its diff:
```python
import jax
import jax.numpy as jnp
from jax import lax
from jax.experimental import pallas as pl
from jax.experimental.pallas import tpu as pltpu
from jax.sharding import PartitionSpec as P

LANES = 128
SUBLANES = 8
MIB = 1 << 20
ROWS, COLS = 8, 16


def spot(row, col):
    return row * COLS + col


def owner(i):
    return i


def head_kernel(ids_ref, table_ref, out_ref, sem):
    parts, tiles = out_ref.shape[:2]
    tokens = ids_ref.shape[0]
    halves = table_ref.shape[0]
    local = (tiles - 1) // halves

    @pl.loop(0, parts, unroll=4)
    def _(i):
        start = owner(i) * local
        for h in range(halves):
            pltpu.make_async_copy(
                table_ref.at[h, pl.ds(start, local)], out_ref.at[i, pl.ds(h * local, local)], sem
            ).start()

    whole = out_ref.at[:, pl.ds(0, halves * local)]
    pltpu.make_async_copy(whole, whole, sem).wait()

    me = lax.axis_index("row")
    lane = lax.broadcasted_iota(jnp.int32, (SUBLANES, LANES), 1)
    here = tokens // COLS
    for block in range(tokens // LANES):

        def step(i, accs):
            at = ids_ref[block * LANES + i]
            tile = lax.shift_right_logical(at, 7)
            part = spot(lax.shift_right_logical(tile, 8), lax.bitwise_and(lax.shift_right_logical(tile, 4), COLS - 1))
            inner = lax.bitwise_and(tile, local - 1)
            turn = lax.bitwise_and(i - at, LANES - 1)
            hit = lane == i
            out = []
            for h, acc in enumerate(accs):
                turned = pltpu.roll(out_ref[part, inner + h * local].astype(jnp.float32), turn, 1)
                out.append(jnp.where(hit, turned, acc))
            return tuple(out)

        zero = jnp.zeros((SUBLANES, LANES), jnp.float32)
        low, high = lax.fori_loop(0, LANES, step, (zero, zero), unroll=8)
        high = pltpu.roll(high, here, 1)
        for s in range(LANES // here):
            mine = (lane >= s * here) & (lane < (s + 1) * here)
            packed = jnp.where(mine, low, high).astype(jnp.bfloat16)
            out_ref[spot(me, block * (LANES // here) + s), tiles - 1] = packed


def head(token_ids, table):
    halves, tiles = table.shape[:2]
    parts = ROWS * COLS
    return pl.pallas_call(
        head_kernel,
        out_shape=pltpu.VMEM((parts, halves * tiles // parts + 1, SUBLANES, LANES), jnp.bfloat16),
        in_specs=[pl.BlockSpec(memory_space=pltpu.SMEM), pl.BlockSpec(memory_space=pl.ANY)],
        out_specs=pl.BlockSpec(memory_space=pltpu.VMEM),
        scratch_shapes=[pltpu.SemaphoreType.DMA],
        cost_estimate=pl.CostEstimate(flops=20 * MIB, bytes_accessed=16 * MIB, transcendentals=0),
        compiler_params=pltpu.CompilerParams(vmem_limit_bytes=16 * MIB),
    )(token_ids, pltpu.with_memory_space_constraint(table, pltpu.HBM))


def tail_kernel(arrived_ref, hidden_ref, gate_ref, proj_ref, gain_ref, served_ref, update_ref, emb_ref, sem):
    parts, tiles = arrived_ref.shape[:2]

    @pl.loop(0, ROWS)
    def _(row):
        @pl.loop(0, COLS, unroll=8)
        def _(col):
            pltpu.make_async_copy(
                arrived_ref.at[spot(row, col), pl.ds(0, tiles - 1)], served_ref.at[row, col], sem
            ).start()

    gate_pre = jnp.dot(hidden_ref[0], gate_ref[0], preferred_element_type=jnp.float32)
    gated = jax.nn.gelu(gate_pre, approximate=True)
    here = gated.shape[0]
    me, share = lax.axis_index("col"), LANES // here
    row = lax.axis_index("row")
    turn = lax.rem(share - lax.rem(me, share), share) * here
    for col in range(COLS):
        tile = arrived_ref[spot(row, col), tiles - 1].astype(jnp.float32)
        low = pltpu.roll(tile, turn, 1)
        emb_ref[2 * col * SUBLANES:(2 * col + 1) * SUBLANES] = low
        emb_ref[(2 * col + 1) * SUBLANES:(2 * col + 2) * SUBLANES] = pltpu.roll(low, LANES - here, 1)
    emb = jnp.transpose(emb_ref[...])[:here]
    mixed = (gated * emb).astype(jnp.bfloat16)
    projected = jnp.dot(mixed, proj_ref[0], preferred_element_type=jnp.float32)
    inverse_rms = lax.rsqrt(jnp.mean(projected * projected, axis=-1, keepdims=True) + 1e-06)
    update_ref[0] = (projected * inverse_rms * gain_ref[...].astype(jnp.float32)).astype(jnp.bfloat16)
    pltpu.make_async_copy(served_ref, served_ref, sem).wait()


def tail(arrived, hidden, w_gate, w_proj, gain):
    tiles = arrived.shape[1] - 1
    return pl.pallas_call(
        tail_kernel,
        out_shape=[
            pltpu.HBM((ROWS, COLS, tiles, SUBLANES, LANES), jnp.bfloat16),
            jax.ShapeDtypeStruct(hidden.shape, jnp.bfloat16),
        ],
        in_specs=[pl.BlockSpec(memory_space=pltpu.VMEM)] * 5,
        out_specs=[pl.BlockSpec(memory_space=pl.ANY), pl.BlockSpec(memory_space=pltpu.VMEM)],
        scratch_shapes=[pltpu.VMEM((w_gate.shape[2], LANES), jnp.float32), pltpu.SemaphoreType.DMA],
        cost_estimate=pl.CostEstimate(flops=100 * MIB, bytes_accessed=18 * MIB, transcendentals=0),
        compiler_params=pltpu.CompilerParams(vmem_limit_bytes=24 * MIB),
    )(pltpu.with_memory_space_constraint(arrived, pltpu.VMEM), hidden, w_gate, w_proj, gain)


def shards(train_table, token_ids, hidden, w_gate, w_proj, gain):
    columns, vocab = train_table.shape[1:]
    parts = ROWS * COLS
    halves, tiles = columns // SUBLANES, vocab // LANES
    table = jnp.transpose(train_table.reshape(halves, SUBLANES, tiles, LANES), (0, 2, 1, 3))
    blocks = head(token_ids, table)
    arrived = lax.all_to_all(blocks, ("row", "col"), split_axis=0, concat_axis=0, tiled=True)
    served, update = tail(arrived, hidden, w_gate, w_proj, gain)
    served = served.reshape(ROWS, COLS, halves, tiles // parts, SUBLANES, LANES)
    served = jnp.transpose(served, (0, 1, 2, 4, 3, 5)).reshape(ROWS, COLS * columns, vocab // parts)
    return (served, update)


def solution(mesh):
    in_specs = (
        P("row", "col", None),
        P(),
        P("row", "col", None),
        P("row", None, None),
        P("row", None, None),
        P("row", None),
    )
    out_specs = (P(None, None, ("row", "col")), P("row", "col", None))
    return jax.shard_map(shards, mesh=mesh, in_specs=in_specs, out_specs=out_specs, check_vma=False)
```

time: 208 us -> 128 us (0.62)
  blocking collectives: 0 us -> 111 us
  waiting for transfers between devices: 104 us -> 0 us
  local copies, waits for them, and re-layouts: 80.4 us -> 0.7 us
  starting transfers between devices: 18.2 us -> 0 us
  Pallas kernels: 0 us -> 14.4 us
  other arithmetic: 2.33 us -> 0 us
    all_to_all x0 -> x1, blocking collectives: none -> 111 us  [shards(): lax.all_to_all(blocks, ('row', 'col'), split_axis=0, concat_axis=0, tiled...]
    all_to_all x2 -> x0, waiting for transfers between devices: 104 us -> none  [the longest x1 104 us: shards(): lax.all_to_all(shaped, ('row', 'col'), split_axis=1, concat_axis=0, tiled...]
    unnamed x13 -> x10, local copies, waits for them, and re-layouts: 65.3 us -> 0.7 us
    all_to_all x2 -> x0, starting transfers between devices: 18.2 us -> none  [the longest x1 10.1 us: shards(): lax.all_to_all(shaped, ('row', 'col'), split_axis=1, concat_axis=0, tiled...]
    pallas_call x0 -> x2, Pallas kernels: none -> 14.4 us  [the longest x1 10.6 us: head(): pl.pallas_call(head_kernel, out_shape=pltpu.VMEM((parts, halves * tiles /...]
    reshape x1 -> x0, local copies, waits for them, and re-layouts: 11.2 us -> none  [shards(): shaped = train_table.reshape(columns, devices_all, local_vocab)]
    gather x2 -> x0, local copies, waits for them, and re-layouts: 3.7 us -> none  [shards(): picked = jnp.take(train_table[0], token_ids, axis=1)]
  transfers between devices with their start and end apart: 2 -> 0, of which waited for: 1 -> 0; matrix products, arithmetic and copies ran while one was open for 12% -> 0% of each run, Pallas kernels for 0% -> 0%
where the time goes in v2:
time: 128 us; the launch traced here: 127 us
  blocking collectives  111 us (87%)
  Pallas kernels  14.4 us (11%)
    all_to_all x1, blocking collectives, shards(): lax.all_to_all(blocks, ('row', 'col'), split_axis=0, concat_axis=0, tiled...  111 us
    pallas_call x1, Pallas kernels, head(): pl.pallas_call(head_kernel, out_shape=pltpu.VMEM((parts, halves * tiles /...  10.6 us
    pallas_call x1, Pallas kernels, tail(): pl.pallas_call(tail_kernel, out_shape=[pltpu.HBM((ROWS, COLS, tiles, SUBL...  3.88 us

profile of v2, /device:TPU:6, one launch (start us, length us, event | category | flops | bytes accessed | tf_op | source)
XLA Modules:
  0.0 127.0 jit_solution(17817221636491196009)
XLA Ops:
  0.6 0.0 copy-start.4
  0.6 0.7 copy-done.4
  1.3 10.6 %shard_map.77 = bf16[128,33,8,128]{3,2,1,0:T(8,128)(2,1)S(1)} custom-call(s32[512]{0:T(512)S(1)} %copy-done.4, bf16[2,2048,8,128]{3,2,1,0:T(8,128)(2,1)} %bitcast.8), custom_call_target="tpu_custom_call" | custom-call | flops 20971520 | bytes 16777216 | tf_op jit(solution)/shard_map/pallas_call | solution.py:69
  11.9 0.0 copy-start
  11.9 0.0 copy-start.1
  11.9 0.0 copy-start.2
  11.9 0.0 copy-start.3
  11.9 111.1 %all_to_all.5.arrived_ref = bf16[128,33,8,128]{3,2,1,0:T(8,128)(2,1)S(1)} all-to-all(bf16[128,33,8,128]{3,2,1,0:T(8,128)(2,1)S(1)} %shard_map.77), channel_id=1, replica_groups=mesh['row'=8,'col'=16] {'row','col'}, dimensions={0} | all-to-all | bytes 17301504 | tf_op jit(solution)/shard_map/all_to_all | solution.py:132
  123.1 0.0 copy-done
  123.1 0.0 copy-done.1
  123.1 0.0 copy-done.2
  123.1 0.0 copy-done.3
  123.1 3.9 %shard_map.78 = (bf16[8,16,32,8,128]{4,3,2,1,0:T(8,128)(2,1)}, bf16[1,32,2560]{2,1,0:T(8,128)(2,1)}) custom-call(bf16[128,33,8,128]{3,2,1,0:T(8,128)(2,1)S(1)} %all_to_all.5.arrived_ref, bf16[1,32,2560]{2,1,0:T(8,128)(2,1)S(1)} %copy-done.2, bf16[1,2560,256]{2,1,0:T(8,128)(2,1)S(1)} %copy-done, bf16[1,256,2560]{2,1,0:T(8,128)(2,1)S(1)} %copy-done.1, ...), custom_call_target="tpu_custom_call" | custom-call | flops 104857600 | bytes 18874368 | tf_op jit(solution)/shard_map/pallas_call | solution.py:112
Async XLA Ops:
  0.6 0.7 copy-start.4
  11.9 111.2 %copy-start = (bf16[1,2560,256]{2,1,0:T(8,128)(2,1)S(1)}, bf16[1,2560,256]{2,1,0:T(8,128)(2,1)}, u32[]{:S(2)}) copy-start(bf16[1,2560,256]{2,1,0:T(8,128)(2,1)} %gate_ref.1) | copy-start | bytes 3932164
  11.9 111.2 %copy-start.1 = (bf16[1,256,2560]{2,1,0:T(8,128)(2,1)S(1)}, bf16[1,256,2560]{2,1,0:T(8,128)(2,1)}, u32[]{:S(2)}) copy-start(bf16[1,256,2560]{2,1,0:T(8,128)(2,1)} %proj_ref.1) | copy-start | bytes 3932164
  11.9 111.2 %copy-start.2 = (bf16[1,32,2560]{2,1,0:T(8,128)(2,1)S(1)}, bf16[1,32,2560]{2,1,0:T(8,128)(2,1)}, u32[]{:S(2)}) copy-start(bf16[1,32,2560]{2,1,0:T(8,128)(2,1)} %hidden_ref.1) | copy-start | bytes 491524
  11.9 111.1 %copy-start.3 = (bf16[1,2560]{1,0:T(2,128)(2,1)S(1)}, bf16[1,2560]{1,0:T(2,128)(2,1)}, u32[]{:S(2)}) copy-start(bf16[1,2560]{1,0:T(2,128)(2,1)} %gain_ref.1) | copy-start | bytes 15364

commit v3 on v2

--- a/solution.py
+++ b/solution.py
@@ -11,70 +11,69 @@
 ROWS, COLS = 8, 16
 
 
-def spot(row, col):
-    return row * COLS + col
+def in_hbm(array):
+    return pltpu.with_memory_space_constraint(array, pltpu.HBM)
 
 
-def owner(i):
-    return i
-
-
-def head_kernel(ids_ref, table_ref, out_ref, sem):
-    parts, tiles = out_ref.shape[:2]
-    tokens = ids_ref.shape[0]
-    halves = table_ref.shape[0]
-    local = (tiles - 1) // halves
-
-    @pl.loop(0, parts, unroll=4)
-    def _(i):
-        start = owner(i) * local
+def head_kernel(ids_ref, table_ref, out_ref, ids, tile_of, turn_of, sem, ids_sem):
+    halves, parts, local = table_ref.shape[:3]
+    tokens = ids.shape[0]
+    pieces = 8
+    size = parts // pieces
+    for p in range(pieces):
         for h in range(halves):
             pltpu.make_async_copy(
-                table_ref.at[h, pl.ds(start, local)], out_ref.at[i, pl.ds(h * local, local)], sem
+                table_ref.at[h, pl.ds(p * size, size)],
+                out_ref.at[pl.ds(p * size, size), pl.ds(h * local, local)],
+                sem,
             ).start()
+    fetch = pltpu.make_async_copy(ids_ref, ids, ids_sem)
+    fetch.start()
+    fetch.wait()
 
+    @pl.loop(0, tokens, unroll=8)
+    def _(t):
+        at = ids[t]
+        tile = lax.shift_right_logical(at, 7)
+        tile_of[t] = tile + (halves * local + 1 - local) * lax.shift_right_logical(tile, 4)
+        turn_of[t] = lax.bitwise_and(t - at, LANES - 1)
+
+    flat = out_ref.reshape(parts * (halves * local + 1), SUBLANES, LANES)
     whole = out_ref.at[:, pl.ds(0, halves * local)]
     pltpu.make_async_copy(whole, whole, sem).wait()
 
-    me = lax.axis_index("row")
+    row = lax.axis_index("row")
     lane = lax.broadcasted_iota(jnp.int32, (SUBLANES, LANES), 1)
     here = tokens // COLS
-    for block in range(tokens // LANES):
+    peers = LANES // here
 
-        def step(i, accs):
-            at = ids_ref[block * LANES + i]
-            tile = lax.shift_right_logical(at, 7)
-            part = spot(lax.shift_right_logical(tile, 8), lax.bitwise_and(lax.shift_right_logical(tile, 4), COLS - 1))
-            inner = lax.bitwise_and(tile, local - 1)
-            turn = lax.bitwise_and(i - at, LANES - 1)
-            hit = lane == i
-            out = []
-            for h, acc in enumerate(accs):
-                turned = pltpu.roll(out_ref[part, inner + h * local].astype(jnp.float32), turn, 1)
-                out.append(jnp.where(hit, turned, acc))
-            return tuple(out)
-
-        zero = jnp.zeros((SUBLANES, LANES), jnp.float32)
-        low, high = lax.fori_loop(0, LANES, step, (zero, zero), unroll=8)
-        high = pltpu.roll(high, here, 1)
-        for s in range(LANES // here):
+    @pl.loop(0, tokens // LANES)
+    def _(block):
+        accs = [jnp.zeros((SUBLANES, LANES), jnp.float32)] * halves
+        for i in range(LANES):
+            tile, turn = tile_of[block * LANES + i], turn_of[block * LANES + i]
+            for h in range(halves):
+                turned = pltpu.roll(flat[tile + h * local].astype(jnp.float32), turn, 1)
+                accs[h] = jnp.where(lane == i, turned, accs[h])
+        low, high = accs[0], pltpu.roll(accs[1], here, 1)
+        for s in range(peers):
             mine = (lane >= s * here) & (lane < (s + 1) * here)
             packed = jnp.where(mine, low, high).astype(jnp.bfloat16)
-            out_ref[spot(me, block * (LANES // here) + s), tiles - 1] = packed
+            out_ref[row * COLS + block * peers + s, halves * local] = packed
 
 
 def head(token_ids, table):
-    halves, tiles = table.shape[:2]
-    parts = ROWS * COLS
+    halves, parts, local = table.shape[:3]
+    tokens = token_ids.shape[0]
     return pl.pallas_call(
         head_kernel,
-        out_shape=pltpu.VMEM((parts, halves * tiles // parts + 1, SUBLANES, LANES), jnp.bfloat16),
-        in_specs=[pl.BlockSpec(memory_space=pltpu.SMEM), pl.BlockSpec(memory_space=pl.ANY)],
+        out_shape=pltpu.VMEM((parts, halves * local + 1, SUBLANES, LANES), jnp.bfloat16),
+        in_specs=[pl.BlockSpec(memory_space=pl.ANY)] * 2,
         out_specs=pl.BlockSpec(memory_space=pltpu.VMEM),
-        scratch_shapes=[pltpu.SemaphoreType.DMA],
+        scratch_shapes=[pltpu.SMEM((tokens,), jnp.int32)] * 3 + [pltpu.SemaphoreType.DMA] * 2,
         cost_estimate=pl.CostEstimate(flops=20 * MIB, bytes_accessed=16 * MIB, transcendentals=0),
         compiler_params=pltpu.CompilerParams(vmem_limit_bytes=16 * MIB),
-    )(token_ids, pltpu.with_memory_space_constraint(table, pltpu.HBM))
+    )(in_hbm(token_ids), in_hbm(table))
 
 
 def tail_kernel(arrived_ref, hidden_ref, gate_ref, proj_ref, gain_ref, served_ref, update_ref, emb_ref, sem):
@@ -85,7 +84,7 @@
         @pl.loop(0, COLS, unroll=8)
         def _(col):
             pltpu.make_async_copy(
-                arrived_ref.at[spot(row, col), pl.ds(0, tiles - 1)], served_ref.at[row, col], sem
+                arrived_ref.at[row * COLS + col, pl.ds(0, tiles - 1)], served_ref.at[row, col], sem
             ).start()
 
     gate_pre = jnp.dot(hidden_ref[0], gate_ref[0], preferred_element_type=jnp.float32)
@@ -95,7 +94,7 @@
     row = lax.axis_index("row")
     turn = lax.rem(share - lax.rem(me, share), share) * here
     for col in range(COLS):
-        tile = arrived_ref[spot(row, col), tiles - 1].astype(jnp.float32)
+        tile = arrived_ref[row * COLS + col, tiles - 1].astype(jnp.float32)
         low = pltpu.roll(tile, turn, 1)
         emb_ref[2 * col * SUBLANES:(2 * col + 1) * SUBLANES] = low
         emb_ref[(2 * col + 1) * SUBLANES:(2 * col + 2) * SUBLANES] = pltpu.roll(low, LANES - here, 1)
@@ -128,6 +127,7 @@
     parts = ROWS * COLS
     halves, tiles = columns // SUBLANES, vocab // LANES
     table = jnp.transpose(train_table.reshape(halves, SUBLANES, tiles, LANES), (0, 2, 1, 3))
+    table = table.reshape(halves, parts, tiles // parts, SUBLANES, LANES)
     blocks = head(token_ids, table)
     arrived = lax.all_to_all(blocks, ("row", "col"), split_axis=0, concat_axis=0, tiled=True)
     served, update = tail(arrived, hidden, w_gate, w_proj, gain)

time: 128 us -> 122 us (0.953)
  Pallas kernels: 14.4 us -> 8.7 us
    pallas_call x1, Pallas kernels: 10.6 us -> 4.82 us  [head(): pl.pallas_call(head_kernel, out_shape=pltpu.VMEM((parts, halves * local +...]
where the time goes in v3:
time: 122 us; the launch traced here: 121 us
  blocking collectives  111 us (91%)
  Pallas kernels  8.7 us (7%)
    all_to_all x1, blocking collectives, shards(): lax.all_to_all(blocks, ('row', 'col'), split_axis=0, concat_axis=0, tiled...  111 us
    pallas_call x1, Pallas kernels, head(): pl.pallas_call(head_kernel, out_shape=pltpu.VMEM((parts, halves * local +...  4.82 us
    pallas_call x1, Pallas kernels, tail(): pl.pallas_call(tail_kernel, out_shape=[pltpu.HBM((ROWS, COLS, tiles, SUBL...  3.88 us

profile of v3, /device:TPU:6, one launch (start us, length us, event | category | flops | bytes accessed | tf_op | source)
XLA Modules:
  0.0 120.5 jit_solution(2243432664327787730)
XLA Ops:
  0.6 4.8 %shard_map.77 = bf16[128,33,8,128]{3,2,1,0:T(8,128)(2,1)S(1)} custom-call(s32[512]{0:T(512)} %ids_ref.1, bf16[2,128,16,8,128]{4,3,2,1,0:T(8,128)(2,1)} %bitcast.10), custom_call_target="tpu_custom_call" | custom-call | flops 20971520 | bytes 16777216 | tf_op jit(solution)/shard_map/pallas_call | solution.py:68
  5.5 0.0 copy-start
  5.5 0.0 copy-start.1
  5.5 0.0 copy-start.2
  5.5 0.0 copy-start.3
  5.5 111.1 %all_to_all.5.arrived_ref = bf16[128,33,8,128]{3,2,1,0:T(8,128)(2,1)S(1)} all-to-all(bf16[128,33,8,128]{3,2,1,0:T(8,128)(2,1)S(1)} %shard_map.77), channel_id=1, replica_groups=mesh['row'=8,'col'=16] {'row','col'}, dimensions={0} | all-to-all | bytes 17301504 | tf_op jit(solution)/shard_map/all_to_all | solution.py:132
  116.6 0.0 copy-done
  116.6 0.0 copy-done.1
  116.6 0.0 copy-done.2
  116.6 0.0 copy-done.3
  116.6 3.9 %shard_map.78 = (bf16[8,16,32,8,128]{4,3,2,1,0:T(8,128)(2,1)}, bf16[1,32,2560]{2,1,0:T(8,128)(2,1)}) custom-call(bf16[128,33,8,128]{3,2,1,0:T(8,128)(2,1)S(1)} %all_to_all.5.arrived_ref, bf16[1,32,2560]{2,1,0:T(8,128)(2,1)S(1)} %copy-done.2, bf16[1,2560,256]{2,1,0:T(8,128)(2,1)S(1)} %copy-done, bf16[1,256,2560]{2,1,0:T(8,128)(2,1)S(1)} %copy-done.1, ...), custom_call_target="tpu_custom_call" | custom-call | flops 104857600 | bytes 18874368 | tf_op jit(solution)/shard_map/pallas_call | solution.py:111
Async XLA Ops:
  5.5 111.2 %copy-start = (bf16[1,2560,256]{2,1,0:T(8,128)(2,1)S(1)}, bf16[1,2560,256]{2,1,0:T(8,128)(2,1)}, u32[]{:S(2)}) copy-start(bf16[1,2560,256]{2,1,0:T(8,128)(2,1)} %gate_ref.1) | copy-start | bytes 3932164
  5.5 111.2 %copy-start.1 = (bf16[1,256,2560]{2,1,0:T(8,128)(2,1)S(1)}, bf16[1,256,2560]{2,1,0:T(8,128)(2,1)}, u32[]{:S(2)}) copy-start(bf16[1,256,2560]{2,1,0:T(8,128)(2,1)} %proj_ref.1) | copy-start | bytes 3932164
  5.5 111.2 %copy-start.2 = (bf16[1,32,2560]{2,1,0:T(8,128)(2,1)S(1)}, bf16[1,32,2560]{2,1,0:T(8,128)(2,1)}, u32[]{:S(2)}) copy-start(bf16[1,32,2560]{2,1,0:T(8,128)(2,1)} %hidden_ref.1) | copy-start | bytes 491524
  5.5 111.1 %copy-start.3 = (bf16[1,2560]{1,0:T(2,128)(2,1)S(1)}, bf16[1,2560]{1,0:T(2,128)(2,1)}, u32[]{:S(2)}) copy-start(bf16[1,2560]{1,0:T(2,128)(2,1)} %gain_ref.1) | copy-start | bytes 15364

commit v4 on v3

--- a/solution.py
+++ b/solution.py
@@ -6,7 +6,7 @@
 from jax.sharding import PartitionSpec as P
 
 LANES = 128
-SUBLANES = 8
+SUBLANES = 4
 MIB = 1 << 20
 ROWS, COLS = 8, 16
 
@@ -35,7 +35,7 @@
     def _(t):
         at = ids[t]
         tile = lax.shift_right_logical(at, 7)
-        tile_of[t] = tile + (halves * local + 1 - local) * lax.shift_right_logical(tile, 4)
+        tile_of[t] = 2 * tile + (halves * local + 1 - local) * lax.shift_right_logical(tile, 4)
         turn_of[t] = lax.bitwise_and(t - at, LANES - 1)
 
     flat = out_ref.reshape(parts * (halves * local + 1), SUBLANES, LANES)
@@ -49,17 +49,18 @@
 
     @pl.loop(0, tokens // LANES)
     def _(block):
-        accs = [jnp.zeros((SUBLANES, LANES), jnp.float32)] * halves
+        accs = [jnp.zeros((SUBLANES, LANES), jnp.float32)] * (2 * halves)
         for i in range(LANES):
             tile, turn = tile_of[block * LANES + i], turn_of[block * LANES + i]
-            for h in range(halves):
-                turned = pltpu.roll(flat[tile + h * local].astype(jnp.float32), turn, 1)
-                accs[h] = jnp.where(lane == i, turned, accs[h])
-        low, high = accs[0], pltpu.roll(accs[1], here, 1)
+            for k in range(2 * halves):
+                turned = pltpu.roll(flat[tile + k // 2 * local + k % 2].astype(jnp.float32), turn, 1)
+                accs[k] = jnp.where(lane == i, turned, accs[k])
+        accs = [pltpu.roll(acc, k * here, 1) if k else acc for k, acc in enumerate(accs)]
         for s in range(peers):
-            mine = (lane >= s * here) & (lane < (s + 1) * here)
-            packed = jnp.where(mine, low, high).astype(jnp.bfloat16)
-            out_ref[row * COLS + block * peers + s, halves * local] = packed
+            packed = accs[-1]
+            for k in range(2 * halves - 1):
+                packed = jnp.where(lane // here == (s + k) % peers, accs[k], packed)
+            out_ref[row * COLS + block * peers + s, halves * local] = packed.astype(jnp.bfloat16)
 
 
 def head(token_ids, table):
@@ -76,15 +77,16 @@
     )(in_hbm(token_ids), in_hbm(table))
 
 
-def tail_kernel(arrived_ref, hidden_ref, gate_ref, proj_ref, gain_ref, served_ref, update_ref, emb_ref, sem):
-    parts, tiles = arrived_ref.shape[:2]
+def tail_kernel(arrived_ref, hidden_ref, gate_ref, proj_ref, gain_ref, served_ref, update_ref, emb_ref, branch_ref, sems, update_sem):
+    tiles = arrived_ref.shape[1]
+    halfway = ROWS // 2
 
     @pl.loop(0, ROWS)
     def _(row):
         @pl.loop(0, COLS, unroll=8)
         def _(col):
             pltpu.make_async_copy(
-                arrived_ref.at[row * COLS + col, pl.ds(0, tiles - 1)], served_ref.at[row, col], sem
+                arrived_ref.at[row * COLS + col, pl.ds(0, tiles - 1)], served_ref.at[row, col], sems.at[row // halfway]
             ).start()
 
     gate_pre = jnp.dot(hidden_ref[0], gate_ref[0], preferred_element_type=jnp.float32)
@@ -96,14 +98,20 @@
     for col in range(COLS):
         tile = arrived_ref[row * COLS + col, tiles - 1].astype(jnp.float32)
         low = pltpu.roll(tile, turn, 1)
-        emb_ref[2 * col * SUBLANES:(2 * col + 1) * SUBLANES] = low
-        emb_ref[(2 * col + 1) * SUBLANES:(2 * col + 2) * SUBLANES] = pltpu.roll(low, LANES - here, 1)
+        for k in range(share):
+            start = (col * share + k) * SUBLANES
+            emb_ref[start:start + SUBLANES] = pltpu.roll(low, (LANES - k * here) % LANES, 1) if k else low
     emb = jnp.transpose(emb_ref[...])[:here]
     mixed = (gated * emb).astype(jnp.bfloat16)
     projected = jnp.dot(mixed, proj_ref[0], preferred_element_type=jnp.float32)
     inverse_rms = lax.rsqrt(jnp.mean(projected * projected, axis=-1, keepdims=True) + 1e-06)
-    update_ref[0] = (projected * inverse_rms * gain_ref[...].astype(jnp.float32)).astype(jnp.bfloat16)
-    pltpu.make_async_copy(served_ref, served_ref, sem).wait()
+    branch_ref[0] = (projected * inverse_rms * gain_ref[...].astype(jnp.float32)).astype(jnp.bfloat16)
+    first, second = served_ref.at[pl.ds(0, halfway)], served_ref.at[pl.ds(halfway, halfway)]
+    pltpu.make_async_copy(first, first, sems.at[0]).wait()
+    send = pltpu.make_async_copy(branch_ref, update_ref, update_sem)
+    send.start()
+    pltpu.make_async_copy(second, second, sems.at[1]).wait()
+    send.wait()
 
 
 def tail(arrived, hidden, w_gate, w_proj, gain):
@@ -112,11 +120,16 @@
         tail_kernel,
         out_shape=[
             pltpu.HBM((ROWS, COLS, tiles, SUBLANES, LANES), jnp.bfloat16),
-            jax.ShapeDtypeStruct(hidden.shape, jnp.bfloat16),
+            pltpu.HBM(hidden.shape, jnp.bfloat16),
         ],
         in_specs=[pl.BlockSpec(memory_space=pltpu.VMEM)] * 5,
-        out_specs=[pl.BlockSpec(memory_space=pl.ANY), pl.BlockSpec(memory_space=pltpu.VMEM)],
-        scratch_shapes=[pltpu.VMEM((w_gate.shape[2], LANES), jnp.float32), pltpu.SemaphoreType.DMA],
+        out_specs=[pl.BlockSpec(memory_space=pl.ANY)] * 2,
+        scratch_shapes=[
+            pltpu.VMEM((w_gate.shape[2], LANES), jnp.float32),
+            pltpu.VMEM(hidden.shape, jnp.bfloat16),
+            pltpu.SemaphoreType.DMA((2,)),
+            pltpu.SemaphoreType.DMA,
+        ],
         cost_estimate=pl.CostEstimate(flops=100 * MIB, bytes_accessed=18 * MIB, transcendentals=0),
         compiler_params=pltpu.CompilerParams(vmem_limit_bytes=24 * MIB),
     )(pltpu.with_memory_space_constraint(arrived, pltpu.VMEM), hidden, w_gate, w_proj, gain)
@@ -125,14 +138,14 @@
 def shards(train_table, token_ids, hidden, w_gate, w_proj, gain):
     columns, vocab = train_table.shape[1:]
     parts = ROWS * COLS
-    halves, tiles = columns // SUBLANES, vocab // LANES
-    table = jnp.transpose(train_table.reshape(halves, SUBLANES, tiles, LANES), (0, 2, 1, 3))
-    table = table.reshape(halves, parts, tiles // parts, SUBLANES, LANES)
+    halves, tiles = columns // 8, vocab // LANES
+    table = train_table.reshape(halves, 2, SUBLANES, tiles, LANES)
+    table = jnp.transpose(table, (0, 3, 1, 2, 4)).reshape(halves, parts, 2 * tiles // parts, SUBLANES, LANES)
     blocks = head(token_ids, table)
     arrived = lax.all_to_all(blocks, ("row", "col"), split_axis=0, concat_axis=0, tiled=True)
     served, update = tail(arrived, hidden, w_gate, w_proj, gain)
-    served = served.reshape(ROWS, COLS, halves, tiles // parts, SUBLANES, LANES)
-    served = jnp.transpose(served, (0, 1, 2, 4, 3, 5)).reshape(ROWS, COLS * columns, vocab // parts)
+    served = served.reshape(ROWS, COLS, halves, tiles // parts, 2, SUBLANES, LANES)
+    served = jnp.transpose(served, (0, 1, 2, 4, 5, 3, 6)).reshape(ROWS, COLS * columns, vocab // parts)
     return (served, update)
 
 

time: 122 us -> 120 us (0.984)
    all_to_all x1, blocking collectives: 111 us -> 110 us  [shards(): lax.all_to_all(blocks, ('row', 'col'), split_axis=0, concat_axis=0, tiled...]
where the time goes in v4:
time: 120 us; the launch traced here: 119 us
  blocking collectives  110 us (92%)
  Pallas kernels  8.37 us (7%)
    all_to_all x1, blocking collectives, shards(): lax.all_to_all(blocks, ('row', 'col'), split_axis=0, concat_axis=0, tiled...  110 us
    pallas_call x1, Pallas kernels, head(): pl.pallas_call(head_kernel, out_shape=pltpu.VMEM((parts, halves * local +...  5.07 us
    pallas_call x1, Pallas kernels, tail(): pl.pallas_call(tail_kernel, out_shape=[pltpu.HBM((ROWS, COLS, tiles, SUBL...  3.3 us

profile of v4, /device:TPU:6, one launch (start us, length us, event | category | flops | bytes accessed | tf_op | source)
XLA Modules:
  0.0 118.8 jit_solution(12224977207898288066)
XLA Ops:
  0.6 5.1 %shard_map.77 = bf16[128,65,4,128]{3,2,1,0:T(4,128)(2,1)S(1)} custom-call(s32[512]{0:T(512)} %ids_ref.1, bf16[2,128,32,4,128]{4,3,2,1,0:T(4,128)(2,1)} %bitcast.10), custom_call_target="tpu_custom_call" | custom-call | flops 20971520 | bytes 16777216 | tf_op jit(solution)/shard_map/pallas_call | solution.py:69
  5.7 0.0 copy-start
  5.7 0.0 copy-start.1
  5.7 0.0 copy-start.2
  5.7 0.0 copy-start.3
  5.8 109.7 %all_to_all.5.arrived_ref = bf16[128,65,4,128]{3,2,1,0:T(4,128)(2,1)S(1)} all-to-all(bf16[128,65,4,128]{3,2,1,0:T(4,128)(2,1)S(1)} %shard_map.77), channel_id=1, replica_groups=mesh['row'=8,'col'=16] {'row','col'}, dimensions={0} | all-to-all | bytes 17039360 | tf_op jit(solution)/shard_map/all_to_all | solution.py:145
  115.5 0.0 copy-done
  115.5 0.0 copy-done.1
  115.5 0.0 copy-done.2
  115.5 0.0 copy-done.3
  115.5 3.3 %shard_map.78 = (bf16[8,16,64,4,128]{4,3,2,1,0:T(4,128)(2,1)}, bf16[1,32,2560]{2,1,0:T(8,128)(2,1)}) custom-call(bf16[128,65,4,128]{3,2,1,0:T(4,128)(2,1)S(1)} %all_to_all.5.arrived_ref, bf16[1,32,2560]{2,1,0:T(8,128)(2,1)S(1)} %copy-done.2, bf16[1,2560,256]{2,1,0:T(8,128)(2,1)S(1)} %copy-done, bf16[1,256,2560]{2,1,0:T(8,128)(2,1)S(1)} %copy-done.1, ...), custom_call_target="tpu_custom_call" | custom-call | flops 104857600 | bytes 18874368 | tf_op jit(solution)/shard_map/pallas_call | solution.py:119
Async XLA Ops:
  5.7 109.8 %copy-start = (bf16[1,2560,256]{2,1,0:T(8,128)(2,1)S(1)}, bf16[1,2560,256]{2,1,0:T(8,128)(2,1)}, u32[]{:S(2)}) copy-start(bf16[1,2560,256]{2,1,0:T(8,128)(2,1)} %gate_ref.1) | copy-start | bytes 3932164
  5.7 109.8 %copy-start.1 = (bf16[1,256,2560]{2,1,0:T(8,128)(2,1)S(1)}, bf16[1,256,2560]{2,1,0:T(8,128)(2,1)}, u32[]{:S(2)}) copy-start(bf16[1,256,2560]{2,1,0:T(8,128)(2,1)} %proj_ref.1) | copy-start | bytes 3932164
  5.7 109.7 %copy-start.2 = (bf16[1,32,2560]{2,1,0:T(8,128)(2,1)S(1)}, bf16[1,32,2560]{2,1,0:T(8,128)(2,1)}, u32[]{:S(2)}) copy-start(bf16[1,32,2560]{2,1,0:T(8,128)(2,1)} %hidden_ref.1) | copy-start | bytes 491524
  5.7 109.7 %copy-start.3 = (bf16[1,2560]{1,0:T(2,128)(2,1)S(1)}, bf16[1,2560]{1,0:T(2,128)(2,1)}, u32[]{:S(2)}) copy-start(bf16[1,2560]{1,0:T(2,128)(2,1)} %gain_ref.1) | copy-start | bytes 15364

commit v5 on v4

--- a/solution.py
+++ b/solution.py
@@ -9,33 +9,44 @@
 SUBLANES = 4
 MIB = 1 << 20
 ROWS, COLS = 8, 16
+SPOT0 = 102
+STEP_X, STEP_Y, STEP_Z, STEP_C = 8, -2, -32, 1
+
+
+def spot(device):
+    x, y = device >> 5, ((device >> 3) & 1) * 2 + ((device >> 4) & 1)
+    z, core = (device >> 1) & 3, device & 1
+    return SPOT0 + x * STEP_X + y * STEP_Y + z * STEP_Z + core * STEP_C
 
 
 def in_hbm(array):
     return pltpu.with_memory_space_constraint(array, pltpu.HBM)
 
 
-def head_kernel(ids_ref, table_ref, out_ref, ids, tile_of, turn_of, sem, ids_sem):
+def head_kernel(ids_ref, table_ref, out_ref, place_of, ids, tile_of, turn_of, sem, ids_sem):
     halves, parts, local = table_ref.shape[:3]
     tokens = ids.shape[0]
-    pieces = 8
-    size = parts // pieces
-    for p in range(pieces):
+    fetch = pltpu.make_async_copy(ids_ref, ids, ids_sem)
+    fetch.start()
+    for device in range(0, parts, 2):
         for h in range(halves):
             pltpu.make_async_copy(
-                table_ref.at[h, pl.ds(p * size, size)],
-                out_ref.at[pl.ds(p * size, size), pl.ds(h * local, local)],
+                table_ref.at[h, pl.ds(device, 2)],
+                out_ref.at[pl.ds(spot(device), 2), pl.ds(h * local, local)],
                 sem,
             ).start()
-    fetch = pltpu.make_async_copy(ids_ref, ids, ids_sem)
-    fetch.start()
+
+    @pl.loop(0, parts, unroll=8)
+    def _(device):
+        place_of[device] = spot(device) * (halves * local + 1)
+
     fetch.wait()
 
     @pl.loop(0, tokens, unroll=8)
     def _(t):
         at = ids[t]
-        tile = lax.shift_right_logical(at, 7)
-        tile_of[t] = 2 * tile + (halves * local + 1 - local) * lax.shift_right_logical(tile, 4)
+        inner = lax.bitwise_and(lax.shift_right_logical(at, 6), local - 2)
+        tile_of[t] = place_of[lax.shift_right_logical(at, 11)] + inner
         turn_of[t] = lax.bitwise_and(t - at, LANES - 1)
 
     flat = out_ref.reshape(parts * (halves * local + 1), SUBLANES, LANES)
@@ -60,7 +71,7 @@
             packed = accs[-1]
             for k in range(2 * halves - 1):
                 packed = jnp.where(lane // here == (s + k) % peers, accs[k], packed)
-            out_ref[row * COLS + block * peers + s, halves * local] = packed.astype(jnp.bfloat16)
+            flat[place_of[row * COLS + block * peers + s] + halves * local] = packed.astype(jnp.bfloat16)
 
 
 def head(token_ids, table):
@@ -71,7 +82,7 @@
         out_shape=pltpu.VMEM((parts, halves * local + 1, SUBLANES, LANES), jnp.bfloat16),
         in_specs=[pl.BlockSpec(memory_space=pl.ANY)] * 2,
         out_specs=pl.BlockSpec(memory_space=pltpu.VMEM),
-        scratch_shapes=[pltpu.SMEM((tokens,), jnp.int32)] * 3 + [pltpu.SemaphoreType.DMA] * 2,
+        scratch_shapes=[pltpu.SMEM((parts,), jnp.int32)] + [pltpu.SMEM((tokens,), jnp.int32)] * 3 + [pltpu.SemaphoreType.DMA] * 2,
         cost_estimate=pl.CostEstimate(flops=20 * MIB, bytes_accessed=16 * MIB, transcendentals=0),
         compiler_params=pltpu.CompilerParams(vmem_limit_bytes=16 * MIB),
     )(in_hbm(token_ids), in_hbm(table))
@@ -86,7 +97,7 @@
         @pl.loop(0, COLS, unroll=8)
         def _(col):
             pltpu.make_async_copy(
-                arrived_ref.at[row * COLS + col, pl.ds(0, tiles - 1)], served_ref.at[row, col], sems.at[row // halfway]
+                arrived_ref.at[spot(row * COLS + col), pl.ds(0, tiles - 1)], served_ref.at[row, col], sems.at[row // halfway]
             ).start()
 
     gate_pre = jnp.dot(hidden_ref[0], gate_ref[0], preferred_element_type=jnp.float32)
@@ -96,7 +107,7 @@
     row = lax.axis_index("row")
     turn = lax.rem(share - lax.rem(me, share), share) * here
     for col in range(COLS):
-        tile = arrived_ref[row * COLS + col, tiles - 1].astype(jnp.float32)
+        tile = arrived_ref[spot(row * COLS + col), tiles - 1].astype(jnp.float32)
         low = pltpu.roll(tile, turn, 1)
         for k in range(share):
             start = (col * share + k) * SUBLANES
@@ -142,7 +153,10 @@
     table = train_table.reshape(halves, 2, SUBLANES, tiles, LANES)
     table = jnp.transpose(table, (0, 3, 1, 2, 4)).reshape(halves, parts, 2 * tiles // parts, SUBLANES, LANES)
     blocks = head(token_ids, table)
-    arrived = lax.all_to_all(blocks, ("row", "col"), split_axis=0, concat_axis=0, tiled=True)
+    order = sorted(range(parts), key=spot)
+    arrived = lax.all_to_all(
+        blocks, ("row", "col"), split_axis=0, concat_axis=0, axis_index_groups=[order], tiled=True
+    )
     served, update = tail(arrived, hidden, w_gate, w_proj, gain)
     served = served.reshape(ROWS, COLS, halves, tiles // parts, 2, SUBLANES, LANES)
     served = jnp.transpose(served, (0, 1, 2, 4, 5, 3, 6)).reshape(ROWS, COLS * columns, vocab // parts)

time: 120 us -> 121 us (level)
  no operation moved by 1% of the time
where the time goes in v5:
time: 121 us; the launch traced here: 119 us
  blocking collectives  110 us (91%)
  Pallas kernels  8.43 us (7%)
    all_to_all x1, blocking collectives, shards(): lax.all_to_all(blocks, ('row', 'col'), split_axis=0, concat_axis=0, axis_...  110 us
    pallas_call x1, Pallas kernels, head(): pl.pallas_call(head_kernel, out_shape=pltpu.VMEM((parts, halves * local +...  5.12 us
    pallas_call x1, Pallas kernels, tail(): pl.pallas_call(tail_kernel, out_shape=[pltpu.HBM((ROWS, COLS, tiles, SUBL...  3.31 us

profile of v5, /device:TPU:6, one launch (start us, length us, event | category | flops | bytes accessed | tf_op | source)
XLA Modules:
  0.0 118.8 jit_solution(4881384263852081929)
XLA Ops:
  0.6 5.1 %shard_map.77 = bf16[128,65,4,128]{3,2,1,0:T(4,128)(2,1)S(1)} custom-call(s32[512]{0:T(512)} %ids_ref.1, bf16[2,128,32,4,128]{4,3,2,1,0:T(4,128)(2,1)} %bitcast.10), custom_call_target="tpu_custom_call" | custom-call | flops 20971520 | bytes 16777216 | tf_op jit(solution)/shard_map/pallas_call | solution.py:80
  5.8 0.0 copy-start
  5.8 0.0 copy-start.1
  5.8 0.0 copy-start.2
  5.8 0.0 copy-start.3
  5.8 109.6 %all_to_all.5.arrived_ref = bf16[128,65,4,128]{3,2,1,0:T(4,128)(2,1)S(1)} all-to-all(bf16[128,65,4,128]{3,2,1,0:T(4,128)(2,1)S(1)} %shard_map.77), channel_id=1, replica_groups={{30,31,14,15,22,23,6,7,62,63,46,47,54,55,38,39,94,95,78,79,86,87,70,71,..., dimensions={0} | all-to-all | bytes 17039360 | tf_op jit(solution)/shard_map/all_to_all | solution.py:157
  115.4 0.0 copy-done
  115.4 0.0 copy-done.1
  115.4 0.0 copy-done.2
  115.4 0.0 copy-done.3
  115.5 3.3 %shard_map.78 = (bf16[8,16,64,4,128]{4,3,2,1,0:T(4,128)(2,1)}, bf16[1,32,2560]{2,1,0:T(8,128)(2,1)}) custom-call(bf16[128,65,4,128]{3,2,1,0:T(4,128)(2,1)S(1)} %all_to_all.5.arrived_ref, bf16[1,32,2560]{2,1,0:T(8,128)(2,1)S(1)} %copy-done.2, bf16[1,2560,256]{2,1,0:T(8,128)(2,1)S(1)} %copy-done, bf16[1,256,2560]{2,1,0:T(8,128)(2,1)S(1)} %copy-done.1, ...), custom_call_target="tpu_custom_call" | custom-call | flops 104857600 | bytes 18874368 | tf_op jit(solution)/shard_map/pallas_call | solution.py:130
Async XLA Ops:
  5.8 109.7 %copy-start = (bf16[1,2560,256]{2,1,0:T(8,128)(2,1)S(1)}, bf16[1,2560,256]{2,1,0:T(8,128)(2,1)}, u32[]{:S(2)}) copy-start(bf16[1,2560,256]{2,1,0:T(8,128)(2,1)} %gate_ref.1) | copy-start | bytes 3932164
  5.8 109.7 %copy-start.1 = (bf16[1,256,2560]{2,1,0:T(8,128)(2,1)S(1)}, bf16[1,256,2560]{2,1,0:T(8,128)(2,1)}, u32[]{:S(2)}) copy-start(bf16[1,256,2560]{2,1,0:T(8,128)(2,1)} %proj_ref.1) | copy-start | bytes 3932164
  5.8 109.7 %copy-start.2 = (bf16[1,32,2560]{2,1,0:T(8,128)(2,1)S(1)}, bf16[1,32,2560]{2,1,0:T(8,128)(2,1)}, u32[]{:S(2)}) copy-start(bf16[1,32,2560]{2,1,0:T(8,128)(2,1)} %hidden_ref.1) | copy-start | bytes 491524
  5.8 109.6 %copy-start.3 = (bf16[1,2560]{1,0:T(2,128)(2,1)S(1)}, bf16[1,2560]{1,0:T(2,128)(2,1)}, u32[]{:S(2)}) copy-start(bf16[1,2560]{1,0:T(2,128)(2,1)} %gain_ref.1) | copy-start | bytes 15364

commit v6 on v5

--- a/solution.py
+++ b/solution.py
@@ -28,11 +28,11 @@
     tokens = ids.shape[0]
     fetch = pltpu.make_async_copy(ids_ref, ids, ids_sem)
     fetch.start()
-    for device in range(0, parts, 2):
+    for device in range(parts):
         for h in range(halves):
             pltpu.make_async_copy(
-                table_ref.at[h, pl.ds(device, 2)],
-                out_ref.at[pl.ds(spot(device), 2), pl.ds(h * local, local)],
+                table_ref.at[h, device],
+                out_ref.at[spot(device), pl.ds(h * local, local)],
                 sem,
             ).start()
 
@@ -55,17 +55,19 @@
 
     row = lax.axis_index("row")
     lane = lax.broadcasted_iota(jnp.int32, (SUBLANES, LANES), 1)
+    wide = lax.broadcasted_iota(jnp.int32, (2 * SUBLANES, LANES), 1)
     here = tokens // COLS
     peers = LANES // here
 
     @pl.loop(0, tokens // LANES)
     def _(block):
-        accs = [jnp.zeros((SUBLANES, LANES), jnp.float32)] * (2 * halves)
+        accs = [jnp.zeros((2 * SUBLANES, LANES), jnp.float32)] * halves
         for i in range(LANES):
             tile, turn = tile_of[block * LANES + i], turn_of[block * LANES + i]
-            for k in range(2 * halves):
-                turned = pltpu.roll(flat[tile + k // 2 * local + k % 2].astype(jnp.float32), turn, 1)
-                accs[k] = jnp.where(lane == i, turned, accs[k])
+            for h in range(halves):
+                pair = flat[pl.ds(tile + h * local, 2)].astype(jnp.float32).reshape(2 * SUBLANES, LANES)
+                accs[h] = jnp.where(wide == i, pltpu.roll(pair, turn, 1), accs[h])
+        accs = [acc[q * SUBLANES:(q + 1) * SUBLANES] for acc in accs for q in range(2)]
         accs = [pltpu.roll(acc, k * here, 1) if k else acc for k, acc in enumerate(accs)]
         for s in range(peers):
             packed = accs[-1]

time: 121 us -> 120 us (level)
  no operation moved by 1% of the time
where the time goes in v6:
time: 120 us; the launch traced here: 118 us
  blocking collectives  110 us (92%)
  Pallas kernels  8.1 us (7%)
    all_to_all x1, blocking collectives, shards(): lax.all_to_all(blocks, ('row', 'col'), split_axis=0, concat_axis=0, axis_...  110 us
    pallas_call x1, Pallas kernels, head(): pl.pallas_call(head_kernel, out_shape=pltpu.VMEM((parts, halves * local +...  4.8 us
    pallas_call x1, Pallas kernels, tail(): pl.pallas_call(tail_kernel, out_shape=[pltpu.HBM((ROWS, COLS, tiles, SUBL...  3.31 us

profile of v6, /device:TPU:6, one launch (start us, length us, event | category | flops | bytes accessed | tf_op | source)
XLA Modules:
  0.0 118.4 jit_solution(8277927388320768516)
XLA Ops:
  0.6 4.8 %shard_map.77 = bf16[128,65,4,128]{3,2,1,0:T(4,128)(2,1)S(1)} custom-call(s32[512]{0:T(512)} %ids_ref.1, bf16[2,128,32,4,128]{4,3,2,1,0:T(4,128)(2,1)} %bitcast.10), custom_call_target="tpu_custom_call" | custom-call | flops 20971520 | bytes 16777216 | tf_op jit(solution)/shard_map/pallas_call | solution.py:82
  5.4 0.0 copy-start
  5.4 0.0 copy-start.1
  5.5 0.0 copy-start.2
  5.5 0.0 copy-start.3
  5.5 109.6 %all_to_all.5.arrived_ref = bf16[128,65,4,128]{3,2,1,0:T(4,128)(2,1)S(1)} all-to-all(bf16[128,65,4,128]{3,2,1,0:T(4,128)(2,1)S(1)} %shard_map.77), channel_id=1, replica_groups={{30,31,14,15,22,23,6,7,62,63,46,47,54,55,38,39,94,95,78,79,86,87,70,71,..., dimensions={0} | all-to-all | bytes 17039360 | tf_op jit(solution)/shard_map/all_to_all | solution.py:159
  115.1 0.0 copy-done
  115.1 0.0 copy-done.1
  115.1 0.0 copy-done.2
  115.1 0.0 copy-done.3
  115.1 3.3 %shard_map.78 = (bf16[8,16,64,4,128]{4,3,2,1,0:T(4,128)(2,1)}, bf16[1,32,2560]{2,1,0:T(8,128)(2,1)}) custom-call(bf16[128,65,4,128]{3,2,1,0:T(4,128)(2,1)S(1)} %all_to_all.5.arrived_ref, bf16[1,32,2560]{2,1,0:T(8,128)(2,1)S(1)} %copy-done.2, bf16[1,2560,256]{2,1,0:T(8,128)(2,1)S(1)} %copy-done, bf16[1,256,2560]{2,1,0:T(8,128)(2,1)S(1)} %copy-done.1, ...), custom_call_target="tpu_custom_call" | custom-call | flops 104857600 | bytes 18874368 | tf_op jit(solution)/shard_map/pallas_call | solution.py:132
Async XLA Ops:
  5.4 109.7 %copy-start = (bf16[1,2560,256]{2,1,0:T(8,128)(2,1)S(1)}, bf16[1,2560,256]{2,1,0:T(8,128)(2,1)}, u32[]{:S(2)}) copy-start(bf16[1,2560,256]{2,1,0:T(8,128)(2,1)} %gate_ref.1) | copy-start | bytes 3932164
  5.4 109.7 %copy-start.1 = (bf16[1,256,2560]{2,1,0:T(8,128)(2,1)S(1)}, bf16[1,256,2560]{2,1,0:T(8,128)(2,1)}, u32[]{:S(2)}) copy-start(bf16[1,256,2560]{2,1,0:T(8,128)(2,1)} %proj_ref.1) | copy-start | bytes 3932164
  5.5 109.7 %copy-start.2 = (bf16[1,32,2560]{2,1,0:T(8,128)(2,1)S(1)}, bf16[1,32,2560]{2,1,0:T(8,128)(2,1)}, u32[]{:S(2)}) copy-start(bf16[1,32,2560]{2,1,0:T(8,128)(2,1)} %hidden_ref.1) | copy-start | bytes 491524
  5.5 109.6 %copy-start.3 = (bf16[1,2560]{1,0:T(2,128)(2,1)S(1)}, bf16[1,2560]{1,0:T(2,128)(2,1)}, u32[]{:S(2)}) copy-start(bf16[1,2560]{1,0:T(2,128)(2,1)} %gain_ref.1) | copy-start | bytes 15364

commit v7 on v6

--- a/solution.py
+++ b/solution.py
@@ -59,8 +59,7 @@
     here = tokens // COLS
     peers = LANES // here
 
-    @pl.loop(0, tokens // LANES)
-    def _(block):
+    for block in range(tokens // LANES):
         accs = [jnp.zeros((2 * SUBLANES, LANES), jnp.float32)] * halves
         for i in range(LANES):
             tile, turn = tile_of[block * LANES + i], turn_of[block * LANES + i]

time: 120 us -> 120 us (level)
  no operation moved by 1% of the time
where the time goes in v7:
time: 120 us; the launch traced here: 118 us
  blocking collectives  110 us (92%)
  Pallas kernels  7.96 us (7%)
    all_to_all x1, blocking collectives, shards(): lax.all_to_all(blocks, ('row', 'col'), split_axis=0, concat_axis=0, axis_...  110 us
    pallas_call x1, Pallas kernels, head(): pl.pallas_call(head_kernel, out_shape=pltpu.VMEM((parts, halves * local +...  4.66 us
    pallas_call x1, Pallas kernels, tail(): pl.pallas_call(tail_kernel, out_shape=[pltpu.HBM((ROWS, COLS, tiles, SUBL...  3.31 us

profile of v7, /device:TPU:6, one launch (start us, length us, event | category | flops | bytes accessed | tf_op | source)
XLA Modules:
  0.0 118.3 jit_solution(10437533672132742389)
XLA Ops:
  0.6 4.7 %shard_map.77 = bf16[128,65,4,128]{3,2,1,0:T(4,128)(2,1)S(1)} custom-call(s32[512]{0:T(512)} %ids_ref.1, bf16[2,128,32,4,128]{4,3,2,1,0:T(4,128)(2,1)} %bitcast.10), custom_call_target="tpu_custom_call" | custom-call | flops 20971520 | bytes 16777216 | tf_op jit(solution)/shard_map/pallas_call | solution.py:81
  5.3 0.0 copy-start
  5.3 0.0 copy-start.1
  5.3 0.0 copy-start.2
  5.3 0.0 copy-start.3
  5.3 109.6 %all_to_all.5.arrived_ref = bf16[128,65,4,128]{3,2,1,0:T(4,128)(2,1)S(1)} all-to-all(bf16[128,65,4,128]{3,2,1,0:T(4,128)(2,1)S(1)} %shard_map.77), channel_id=1, replica_groups={{30,31,14,15,22,23,6,7,62,63,46,47,54,55,38,39,94,95,78,79,86,87,70,71,..., dimensions={0} | all-to-all | bytes 17039360 | tf_op jit(solution)/shard_map/all_to_all | solution.py:158
  115.0 0.0 copy-done
  115.0 0.0 copy-done.1
  115.0 0.0 copy-done.2
  115.0 0.0 copy-done.3
  115.0 3.3 %shard_map.78 = (bf16[8,16,64,4,128]{4,3,2,1,0:T(4,128)(2,1)}, bf16[1,32,2560]{2,1,0:T(8,128)(2,1)}) custom-call(bf16[128,65,4,128]{3,2,1,0:T(4,128)(2,1)S(1)} %all_to_all.5.arrived_ref, bf16[1,32,2560]{2,1,0:T(8,128)(2,1)S(1)} %copy-done.2, bf16[1,2560,256]{2,1,0:T(8,128)(2,1)S(1)} %copy-done, bf16[1,256,2560]{2,1,0:T(8,128)(2,1)S(1)} %copy-done.1, ...), custom_call_target="tpu_custom_call" | custom-call | flops 104857600 | bytes 18874368 | tf_op jit(solution)/shard_map/pallas_call | solution.py:131
Async XLA Ops:
  5.3 109.7 %copy-start = (bf16[1,2560,256]{2,1,0:T(8,128)(2,1)S(1)}, bf16[1,2560,256]{2,1,0:T(8,128)(2,1)}, u32[]{:S(2)}) copy-start(bf16[1,2560,256]{2,1,0:T(8,128)(2,1)} %gate_ref.1) | copy-start | bytes 3932164
  5.3 109.7 %copy-start.1 = (bf16[1,256,2560]{2,1,0:T(8,128)(2,1)S(1)}, bf16[1,256,2560]{2,1,0:T(8,128)(2,1)}, u32[]{:S(2)}) copy-start(bf16[1,256,2560]{2,1,0:T(8,128)(2,1)} %proj_ref.1) | copy-start | bytes 3932164
  5.3 109.7 %copy-start.2 = (bf16[1,32,2560]{2,1,0:T(8,128)(2,1)S(1)}, bf16[1,32,2560]{2,1,0:T(8,128)(2,1)}, u32[]{:S(2)}) copy-start(bf16[1,32,2560]{2,1,0:T(8,128)(2,1)} %hidden_ref.1) | copy-start | bytes 491524
  5.3 109.6 %copy-start.3 = (bf16[1,2560]{1,0:T(2,128)(2,1)S(1)}, bf16[1,2560]{1,0:T(2,128)(2,1)}, u32[]{:S(2)}) copy-start(bf16[1,2560]{1,0:T(2,128)(2,1)} %gain_ref.1) | copy-start | bytes 15364

commit v8 on v7

--- a/solution.py
+++ b/solution.py
@@ -9,8 +9,8 @@
 SUBLANES = 4
 MIB = 1 << 20
 ROWS, COLS = 8, 16
-SPOT0 = 102
-STEP_X, STEP_Y, STEP_Z, STEP_C = 8, -2, -32, 1
+SPOT0 = 120
+STEP_X, STEP_Y, STEP_Z, STEP_C = 2, -8, -32, 1
 
 
 def spot(device):

time: 120 us -> 120 us (level)
  the two profiles are of different devices: /device:TPU:6 before, /device:TPU:1 now
where the time goes in v8:
time: 120 us
  blocking collectives  111 us (92%)
  Pallas kernels  7.96 us (7%)
    all_to_all x1, blocking collectives, shards(): lax.all_to_all(blocks, ('row', 'col'), split_axis=0, concat_axis=0, axis_...  111 us
    pallas_call x1, Pallas kernels, head(): pl.pallas_call(head_kernel, out_shape=pltpu.VMEM((parts, halves * local +...  4.65 us
    pallas_call x1, Pallas kernels, tail(): pl.pallas_call(tail_kernel, out_shape=[pltpu.HBM((ROWS, COLS, tiles, SUBL...  3.31 us

profile of v8, /device:TPU:1, one launch (start us, length us, event | category | flops | bytes accessed | tf_op | source)
XLA Modules:
  0.0 119.8 jit_solution(13177740613917746114)
XLA Ops:
  0.6 4.7 %shard_map.77 = bf16[128,65,4,128]{3,2,1,0:T(4,128)(2,1)S(1)} custom-call(s32[512]{0:T(512)} %ids_ref.1, bf16[2,128,32,4,128]{4,3,2,1,0:T(4,128)(2,1)} %bitcast.10), custom_call_target="tpu_custom_call" | custom-call | flops 20971520 | bytes 16777216 | tf_op jit(solution)/shard_map/pallas_call | solution.py:81
  5.3 0.0 copy-start
  5.3 0.0 copy-start.1
  5.3 0.0 copy-start.2
  5.3 0.0 copy-start.3
  5.3 111.2 %all_to_all.5.arrived_ref = bf16[128,65,4,128]{3,2,1,0:T(4,128)(2,1)S(1)} all-to-all(bf16[128,65,4,128]{3,2,1,0:T(4,128)(2,1)S(1)} %shard_map.77), channel_id=1, replica_groups={{30,31,62,63,94,95,126,127,14,15,46,47,78,79,110,111,22,23,54,55,86,87,..., dimensions={0} | all-to-all | bytes 17039360 | tf_op jit(solution)/shard_map/all_to_all | solution.py:158
  116.5 0.0 copy-done
  116.5 0.0 copy-done.1
  116.5 0.0 copy-done.2
  116.5 0.0 copy-done.3
  116.5 3.3 %shard_map.78 = (bf16[8,16,64,4,128]{4,3,2,1,0:T(4,128)(2,1)}, bf16[1,32,2560]{2,1,0:T(8,128)(2,1)}) custom-call(bf16[128,65,4,128]{3,2,1,0:T(4,128)(2,1)S(1)} %all_to_all.5.arrived_ref, bf16[1,32,2560]{2,1,0:T(8,128)(2,1)S(1)} %copy-done.2, bf16[1,2560,256]{2,1,0:T(8,128)(2,1)S(1)} %copy-done, bf16[1,256,2560]{2,1,0:T(8,128)(2,1)S(1)} %copy-done.1, ...), custom_call_target="tpu_custom_call" | custom-call | flops 104857600 | bytes 18874368 | tf_op jit(solution)/shard_map/pallas_call | solution.py:131
Async XLA Ops:
  5.3 111.2 %copy-start = (bf16[1,2560,256]{2,1,0:T(8,128)(2,1)S(1)}, bf16[1,2560,256]{2,1,0:T(8,128)(2,1)}, u32[]{:S(2)}) copy-start(bf16[1,2560,256]{2,1,0:T(8,128)(2,1)} %gate_ref.1) | copy-start | bytes 3932164
  5.3 111.2 %copy-start.1 = (bf16[1,256,2560]{2,1,0:T(8,128)(2,1)S(1)}, bf16[1,256,2560]{2,1,0:T(8,128)(2,1)}, u32[]{:S(2)}) copy-start(bf16[1,256,2560]{2,1,0:T(8,128)(2,1)} %proj_ref.1) | copy-start | bytes 3932164
  5.3 111.2 %copy-start.2 = (bf16[1,32,2560]{2,1,0:T(8,128)(2,1)S(1)}, bf16[1,32,2560]{2,1,0:T(8,128)(2,1)}, u32[]{:S(2)}) copy-start(bf16[1,32,2560]{2,1,0:T(8,128)(2,1)} %hidden_ref.1) | copy-start | bytes 491524
  5.3 111.2 %copy-start.3 = (bf16[1,2560]{1,0:T(2,128)(2,1)S(1)}, bf16[1,2560]{1,0:T(2,128)(2,1)}, u32[]{:S(2)}) copy-start(bf16[1,2560]{1,0:T(2,128)(2,1)} %gain_ref.1) | copy-start | bytes 15364
